TPU v7x, 32 devices: a whole 2x2x4 slice. The times are simulated.
32 devices in a mesh: gx: 4 (over z), gy: 8 (over y, x, core).
Axes of the slice: x: 2, y: 2, z: 4, core: 2. Of those that a mesh axis runs over, the one named last changes fastest.
Arguments:
- policy_logp: float32 [16, 512, 4096], P('gy', 'gx'), may hold values from -2 to 0
- anchor_logp: float32 [16, 512, 4096], P('gy', 'gx'), may hold values from -2 to 0
- lengths: int32 [16, 512], P('gy', 'gx'), may hold values from 512 to 4096
- rewards: int32 [16, 512], P('gy', 'gx'), may hold values from 0 to 8
- slot_prompt: int32 [16, 512], P('gy', 'gx'), may hold values from 0 to 511, as said below
Outputs:
- token_grad: float32 [16, 512, 4096], P(None, ('gx', 'gy'))
- sample_loss: float32 [16, 512], P(None, ('gx', 'gy'))
- advantage: float32 [16, 512], P(None, ('gx', 'gy'))
Inputs may be any that keep to these rules, and one draw needn't show every extreme that they name: `slot_prompt`: for every member k and every aligned block of 128 slots, the slots of the block hold each prompt of the same block exactly once.
All inputs are finite; a program needn't handle non-finite values.
Results may differ from a plain program's by a relative error of at most 0.00002.
Values sent between devices are 32-bit elements; how exact they have to be, the bound alone decides.
A program may use at most 64 MiB of HBM per device.

v0:
```python
import jax
import jax.numpy as jnp
from jax import lax
from jax.sharding import PartitionSpec as P

kl_weight = 0.1


def score_tokens(policy, anchor, seq_len, reward, total, members, grad_scale, loss_scale):
    advantage = (members * reward - total[None, :]) / (members - 1)
    positions = lax.broadcasted_iota(jnp.float32, policy.shape, 2)
    valid = positions < seq_len[:, :, None]
    log_ratio = anchor - policy
    ratio = jnp.exp(log_ratio)
    token_term = -advantage[:, :, None] * policy + kl_weight * (ratio - log_ratio - 1.0)
    token_grad = (
        jnp.where(valid, -advantage[:, :, None] + kl_weight * (1.0 - ratio), 0.0) * grad_scale
    )
    sample_loss = jnp.sum(jnp.where(valid, token_term, 0.0), axis=2) * loss_scale
    return (token_grad, sample_loss, advantage)


def body(policy_logp, anchor_logp, lengths, rewards, slot_prompt):
    members_dev, slots, seq_slots = policy_logp.shape
    local_prompt = slot_prompt % slots
    member_rows = lax.broadcasted_iota(jnp.int32, (members_dev, slots), 0)
    slot_ids = lax.broadcasted_iota(jnp.int32, (members_dev, slots), 1)
    inverse = jnp.zeros((members_dev, slots), jnp.int32).at[member_rows, local_prompt].set(slot_ids)
    sorted_policy = jnp.take_along_axis(policy_logp, inverse[:, :, None], axis=1)
    sorted_anchor = jnp.take_along_axis(anchor_logp, inverse[:, :, None], axis=1)
    sorted_len = jnp.take_along_axis(lengths, inverse, axis=1).astype(jnp.float32)
    sorted_reward = jnp.take_along_axis(rewards, inverse, axis=1).astype(jnp.float32) * 0.25
    count_local = jnp.sum(lengths.astype(jnp.float32))
    token_total = lax.psum(count_local, ("gx", "gy"))
    members = members_dev * lax.axis_size("gy")
    samples = members * slots * lax.axis_size("gx")
    grad_scale = samples * seq_slots / token_total
    loss_scale = samples / token_total
    member_sums = jnp.sum(sorted_reward, axis=0)
    total = lax.psum(member_sums, "gy")
    token_grad, sample_loss, advantage = score_tokens(
        sorted_policy,
        sorted_anchor,
        sorted_len,
        sorted_reward,
        total,
        members,
        grad_scale,
        loss_scale,
    )
    return (
        lax.all_to_all(token_grad, "gy", split_axis=1, concat_axis=0, tiled=True),
        lax.all_to_all(sample_loss, "gy", split_axis=1, concat_axis=0, tiled=True),
        lax.all_to_all(advantage, "gy", split_axis=1, concat_axis=0, tiled=True),
    )


def solution(mesh):
    placed = (P("gy", "gx", None), P("gy", "gx", None), P("gy", "gx"), P("gy", "gx"), P("gy", "gx"))
    return jax.shard_map(
        body,
        mesh=mesh,
        in_specs=placed,
        out_specs=(P(None, ("gx", "gy"), None), P(None, ("gx", "gy")), P(None, ("gx", "gy"))),
        check_vma=False,
    )
```

profile of v0, /device:TPU:0, one launch (start us, length us, event | category | flops | bytes accessed | tf_op | source)
XLA Modules:
  0.0 189.2 jit_solution(11175729835720736867)
XLA Ops:
  0.6 0.0 copy-start
  0.7 0.7 fusion.16
  1.4 11.4 %scatter_fusion = s32[2,128]{1,0:T(2,128)S(1)} fusion(s32[2,128]{1,0:T(2,128)S(1)} %broadcast.49, s32[256]{0:T(256)S(1)} %fusion.16, s32[256]{0:T(256)S(1)} %iota_bitcast_fusion), kind=kCustom, calls=%fused_computation.4 | custom fusion | bytes 5120 | tf_op jit(solution)/shard_map/scatter | solution.py:28
  12.8 1.3 convert_reduce_fusion
  14.1 2.3 %gather_fusion = s32[256]{0:T(256)S(1)} fusion(s32[2,128]{1,0:T(2,128)} %param.11, s32[256]{0:T(256)S(1)} %get-tuple-element.10), kind=kCustom, calls=%fused_computation.clone | custom fusion | bytes 4096 | tf_op jit(solution)/shard_map/jit(take_along_axis)/gather | solution.py:31
  16.5 0.0 copy-done
  16.5 2.4 %gather_fusion.1 = s32[256]{0:T(256)S(1)} fusion(s32[2,128]{1,0:T(2,128)S(1)} %copy-done, s32[256]{0:T(256)S(1)} %get-tuple-element.10), kind=kCustom, calls=%fused_computation.2.clone | custom fusion | bytes 4096 | tf_op jit(solution)/shard_map/jit(take_along_axis)/gather | solution.py:32
  18.9 15.1 %psum.14 = f32[128]{0:T(128)S(1)} all-reduce(f32[128]{0:T(128)S(1)} %multiply_reduce_fusion), channel_id=1, replica_groups=mesh['gx'=4,'gy'=8] {'gy'}, use_global_device_ids=true, to_apply=%region_2.4 | all-reduce | flops 128 | bytes 1024 | tf_op jit(solution)/shard_map/psum | solution.py:40
  34.1 0.1 copy.35
  34.2 0.1 copy.34
  34.3 7.6 %gather_fusion.2 = f32[256,4096]{1,0:T(8,128)} fusion(f32[2,128,4096]{2,1,0:T(8,128)} %param.10, s32[256]{0:T(256)S(1)} %get-tuple-element.9), kind=kCustom, calls=%fused_computation.1.clone | custom fusion | bytes 8390656 | tf_op jit(solution)/shard_map/jit(take_along_axis)/gather | solution.py:30
  41.9 7.6 %gather_fusion.3 = f32[256,4096]{1,0:T(8,128)} fusion(f32[2,128,4096]{2,1,0:T(8,128)} %param.9, s32[256]{0:T(256)S(1)} %get-tuple-element.9), kind=kCustom, calls=%fused_computation.3.clone | custom fusion | bytes 8390656 | tf_op jit(solution)/shard_map/jit(take_along_axis)/gather | solution.py:29
  49.5 0.1 copy.36
  49.7 39.9 %psum.15 = f32[]{:T(128)} all-reduce(f32[]{:T(128)} %convert_reduce_fusion), channel_id=1, replica_groups=mesh['gx'=4,'gy'=8] {'gx','gy'}, use_global_device_ids=true, to_apply=%region_4.7 | all-reduce | flops 1 | bytes 8 | tf_op jit(solution)/shard_map/psum | solution.py:34
  90.9 20.6 %fusion.9 = (f32[2,128]{0,1:T(8,128)S(1)}, f32[2,128,4096]{2,0,1:T(2,128)}) fusion(f32[2,128,4096]{2,1,0:T(8,128)} %bitcast.49, pred[2,128]{0,1:T(8,128)(4,1)S(1)} %copy.36, f32[2,128]{0,1:T(8,128)S(1)} %copy.35, f32[2,128]{0,1:T(8,128)S(1)} %copy.34, f32[2,128,4096]{2,1,0:T(8,128)} %bitcast.48, f32[]{:T(128)S(6)} %div.14), kind=kLoop, calls=%fused_computation.19 | loop fusion | flops 16776960 | bytes 12586244 | tf_op jit(solution)/shard_map/reduce_sum | solution.py:19
  111.5 0.7 copy.42
  112.2 3.8 %all-to-all-start.1 = ((f32[2,8,16]{2,0,1:T(2,128)}), f32[2,8,16]{2,0,1:T(2,128)S(1)}, u32[]{:S(2)}, u32[]{:S(2)}) async-start(f32[2,8,16]{2,0,1:T(2,128)} %copy.42), calls=%async_computation.1 | async-start | bytes 16384 | tf_op jit(solution)/shard_map/all_to_all | solution.py:53
  116.0 0.1 all_to_all.46
  116.1 4.6 %all-to-all-done.1 = f32[2,8,16]{2,0,1:T(2,128)S(1)} async-done(((f32[2,8,16]{2,0,1:T(2,128)}), f32[2,8,16]{2,0,1:T(2,128)S(1)}, u32[]{:S(2)}, u32[]{:S(2)}) %all-to-all-start.1) | async-done | bytes 1056 | tf_op jit(solution)/shard_map/all_to_all | solution.py:53
  120.7 7.1 %all_to_all.53 = f32[2,8,16]{2,0,1:T(2,128)S(1)} all-to-all(f32[2,8,16]{2,0,1:T(2,128)S(1)} %copy.43), channel_id=1, replica_groups=mesh['gx'=4,'gy'=8] {'gy'}, dimensions={1} | all-to-all | bytes 2048 | tf_op jit(solution)/shard_map/all_to_all | solution.py:54
  127.8 4.5 %all-to-all-start = ((f32[2,128,4096]{2,0,1:T(2,128)}), f32[2,128,4096]{2,0,1:T(2,128)}, u32[]{:S(2)}, u32[]{:S(2)}) async-start(f32[2,128,4096]{2,0,1:T(2,128)} %get-tuple-element.8), calls=%async_computation | async-start | bytes 8388608 | tf_op jit(solution)/shard_map/all_to_all | solution.py:52
  132.3 49.1 %all-to-all-done = f32[2,128,4096]{2,0,1:T(2,128)} async-done(((f32[2,128,4096]{2,0,1:T(2,128)}), f32[2,128,4096]{2,0,1:T(2,128)}, u32[]{:S(2)}, u32[]{:S(2)}) %all-to-all-start) | async-done | bytes 4194336 | tf_op jit(solution)/shard_map/all_to_all | solution.py:52
  181.4 6.6 %copy.40 = f32[8,2,16,4096]{3,2,1,0:T(8,128)} copy(f32[8,2,16,4096]{3,1,2,0:T(2,128)} %bitcast.13) | data formatting | bytes 8388608 | tf_op jit(solution)/shard_map/all_to_all | solution.py:52
  188.0 0.6 copy.66
  188.6 0.6 copy.67
  (9 shorter events, 0.1 us)
Async XLA Ops:
  0.6 15.8 %copy-start = (s32[2,128]{1,0:T(2,128)S(1)}, s32[2,128]{1,0:T(2,128)}, u32[]{:S(2)}) copy-start(s32[2,128]{1,0:T(2,128)} %param.12) | copy-start | bytes 3076
  112.2 8.5 %all-to-all-start.1 = ((f32[2,8,16]{2,0,1:T(2,128)}), f32[2,8,16]{2,0,1:T(2,128)S(1)}, u32[]{:S(2)}, u32[]{:S(2)}) async-start(f32[2,8,16]{2,0,1:T(2,128)} %copy.42), calls=%async_computation.1 | async-start | bytes 16384 | tf_op jit(solution)/shard_map/all_to_all | solution.py:53
  127.8 53.7 %all-to-all-start = ((f32[2,128,4096]{2,0,1:T(2,128)}), f32[2,128,4096]{2,0,1:T(2,128)}, u32[]{:S(2)}, u32[]{:S(2)}) async-start(f32[2,128,4096]{2,0,1:T(2,128)} %get-tuple-element.8), calls=%async_computation | async-start | bytes 8388608 | tf_op jit(solution)/shard_map/all_to_all | solution.py:52
where the time goes:
time: 190 us; the launch traced here: 189 us
  blocking collectives  62.1 us (33%)
  waiting for transfers between devices  53.7 us (28%)
  local copies, waits for them, and re-layouts  40.4 us (21%)
  other arithmetic  22.6 us (12%)
  starting transfers between devices  8.32 us (4%)
  between operations  2.09 us (1%)
    all_to_all x1, waiting for transfers between devices, body(): lax.all_to_all(token_grad, 'gy', split_axis=1, concat_axis=0, tiled=True)  49.1 us
    psum x1, blocking collectives, body(): token_total = lax.psum(count_local, ('gx', 'gy'))  39.9 us
    reduce_sum x1, other arithmetic, score_tokens(): jnp.sum(jnp.where(valid, token_term, 0.0), axis=2) * loss_scale  20.6 us
    psum x1, blocking collectives, body(): total = lax.psum(member_sums, 'gy')  15.1 us
    scatter x1, local copies, waits for them, and re-layouts, body(): jnp.zeros((members_dev, slots), jnp.int32).at[member_rows, local_prompt]  11.4 us
    gather x1, local copies, waits for them, and re-layouts, body(): jnp.take_along_axis(policy_logp, inverse[:, :, None], axis=1)  7.64 us
    gather x1, local copies, waits for them, and re-layouts, body(): jnp.take_along_axis(anchor_logp, inverse[:, :, None], axis=1)  7.59 us
    all_to_all x1, blocking collectives, body(): lax.all_to_all(advantage, 'gy', split_axis=1, concat_axis=0, tiled=True)  7.06 us
  transfers between devices with their start and end apart: 2, of which 2 were waited for; matrix products, arithmetic and copies ran while one was open for 0% of the time, Pallas kernels for 0%

commit v1 on v0

--- a/solution.py
+++ b/solution.py
@@ -37,7 +37,8 @@
     grad_scale = samples * seq_slots / token_total
     loss_scale = samples / token_total
     member_sums = jnp.sum(sorted_reward, axis=0)
-    total = lax.psum(member_sums, "gy")
+    pieces = lax.all_gather(member_sums, "gy", axis=0, tiled=False)
+    total = pieces.sum(axis=0)
     token_grad, sample_loss, advantage = score_tokens(
         sorted_policy,
         sorted_anchor,

time: 190 us -> 186 us (0.979)
  blocking collectives: 62.1 us -> 57.2 us
    psum x1 -> x0, blocking collectives: 15.1 us -> none  [body(): total = lax.psum(member_sums, 'gy')]
    all_gather x0 -> x1, blocking collectives: none -> 10.3 us  [body(): pieces = lax.all_gather(member_sums, 'gy', axis=0, tiled=False)]
where the time goes in v1:
time: 186 us; the launch traced here: 185 us
  blocking collectives  57.2 us (31%)
  waiting for transfers between devices  53.7 us (29%)
  local copies, waits for them, and re-layouts  40.4 us (22%)
  other arithmetic  22.6 us (12%)
  starting transfers between devices  9.31 us (5%)
  between operations  2.09 us (1%)
    all_to_all x1, waiting for transfers between devices, body(): lax.all_to_all(token_grad, 'gy', split_axis=1, concat_axis=0, tiled=True)  49.1 us
    psum x1, blocking collectives, body(): token_total = lax.psum(count_local, ('gx', 'gy'))  39.9 us
    reduce_sum x1, other arithmetic, score_tokens(): jnp.sum(jnp.where(valid, token_term, 0.0), axis=2) * loss_scale  20.6 us
    scatter x1, local copies, waits for them, and re-layouts, body(): jnp.zeros((members_dev, slots), jnp.int32).at[member_rows, local_prompt]  11.4 us
    all_gather x1, blocking collectives, body(): pieces = lax.all_gather(member_sums, 'gy', axis=0, tiled=False)  10.3 us
    gather x1, local copies, waits for them, and re-layouts, body(): jnp.take_along_axis(policy_logp, inverse[:, :, None], axis=1)  7.64 us
    gather x1, local copies, waits for them, and re-layouts, body(): jnp.take_along_axis(anchor_logp, inverse[:, :, None], axis=1)  7.59 us
    all_to_all x1, blocking collectives, body(): lax.all_to_all(advantage, 'gy', split_axis=1, concat_axis=0, tiled=True)  7.06 us
  transfers between devices with their start and end apart: 2, of which 2 were waited for; matrix products, arithmetic and copies ran while one was open for 0% of the time, Pallas kernels for 0%

profile of v1, /device:TPU:0, one launch (start us, length us, event | category | flops | bytes accessed | tf_op | source)
XLA Modules:
  0.0 185.3 jit_solution(11010620639445221697)
XLA Ops:
  0.6 0.0 copy-start
  0.7 0.7 fusion.16
  1.4 11.4 %scatter_fusion = s32[2,128]{1,0:T(2,128)S(1)} fusion(s32[2,128]{1,0:T(2,128)S(1)} %broadcast.49, s32[256]{0:T(256)S(1)} %fusion.16, s32[256]{0:T(256)S(1)} %iota_bitcast_fusion), kind=kCustom, calls=%fused_computation.4 | custom fusion | bytes 5120 | tf_op jit(solution)/shard_map/scatter | solution.py:28
  12.8 1.3 convert_reduce_fusion
  14.1 2.3 %gather_fusion = s32[256]{0:T(256)S(1)} fusion(s32[2,128]{1,0:T(2,128)} %param.11, s32[256]{0:T(256)S(1)} %get-tuple-element.10), kind=kCustom, calls=%fused_computation.clone | custom fusion | bytes 4096 | tf_op jit(solution)/shard_map/jit(take_along_axis)/gather | solution.py:31
  16.5 0.0 copy-done
  16.5 2.4 %gather_fusion.1 = s32[256]{0:T(256)S(1)} fusion(s32[2,128]{1,0:T(2,128)S(1)} %copy-done, s32[256]{0:T(256)S(1)} %get-tuple-element.10), kind=kCustom, calls=%fused_computation.2.clone | custom fusion | bytes 4096 | tf_op jit(solution)/shard_map/jit(take_along_axis)/gather | solution.py:32
  18.9 10.3 %all-gather.1 = f32[8,1,128]{2,1,0:T(1,128)S(1)} all-gather(f32[1,1,128]{2,1,0:T(1,128)S(1)} %bitcast.55), channel_id=2, replica_groups=mesh['gx'=4,'gy'=8] {'gy'}, dimensions={0}, use_global_device_ids=true | all-gather | bytes 4608 | tf_op jit(solution)/shard_map/all_gather | solution.py:40
  29.2 0.1 copy.35
  29.4 0.1 copy.34
  29.5 7.6 %gather_fusion.2 = f32[256,4096]{1,0:T(8,128)} fusion(f32[2,128,4096]{2,1,0:T(8,128)} %param.10, s32[256]{0:T(256)S(1)} %get-tuple-element.9), kind=kCustom, calls=%fused_computation.1.clone | custom fusion | bytes 8390656 | tf_op jit(solution)/shard_map/jit(take_along_axis)/gather | solution.py:30
  37.1 7.6 %gather_fusion.3 = f32[256,4096]{1,0:T(8,128)} fusion(f32[2,128,4096]{2,1,0:T(8,128)} %param.9, s32[256]{0:T(256)S(1)} %get-tuple-element.9), kind=kCustom, calls=%fused_computation.3.clone | custom fusion | bytes 8390656 | tf_op jit(solution)/shard_map/jit(take_along_axis)/gather | solution.py:29
  44.7 0.1 copy.36
  44.8 39.9 %psum.7 = f32[]{:T(128)} all-reduce(f32[]{:T(128)} %convert_reduce_fusion), channel_id=1, replica_groups=mesh['gx'=4,'gy'=8] {'gx','gy'}, use_global_device_ids=true, to_apply=%region_4.7 | all-reduce | flops 1 | bytes 8 | tf_op jit(solution)/shard_map/psum | solution.py:34
  86.1 20.6 %fusion.9 = (f32[2,128]{0,1:T(8,128)S(1)}, f32[2,128,4096]{2,0,1:T(2,128)}) fusion(f32[2,128,4096]{2,1,0:T(8,128)} %bitcast.50, pred[2,128]{0,1:T(8,128)(4,1)S(1)} %copy.36, f32[2,128]{0,1:T(8,128)S(1)} %copy.35, f32[2,128]{0,1:T(8,128)S(1)} %copy.34, f32[2,128,4096]{2,1,0:T(8,128)} %bitcast.49, f32[]{:T(128)S(6)} %div.14), kind=kLoop, calls=%fused_computation.19 | loop fusion | flops 16776960 | bytes 12586244 | tf_op jit(solution)/shard_map/reduce_sum | solution.py:19
  106.6 0.7 copy.42
  107.4 4.8 %all-to-all-start.1 = ((f32[2,8,16]{2,0,1:T(2,128)}), f32[2,8,16]{2,0,1:T(2,128)S(1)}, u32[]{:S(2)}, u32[]{:S(2)}) async-start(f32[2,8,16]{2,0,1:T(2,128)} %copy.42), calls=%async_computation.1 | async-start | bytes 16384 | tf_op jit(solution)/shard_map/all_to_all | solution.py:54
  112.1 0.1 all_to_all.46
  112.2 4.6 %all-to-all-done.1 = f32[2,8,16]{2,0,1:T(2,128)S(1)} async-done(((f32[2,8,16]{2,0,1:T(2,128)}), f32[2,8,16]{2,0,1:T(2,128)S(1)}, u32[]{:S(2)}, u32[]{:S(2)}) %all-to-all-start.1) | async-done | bytes 1056 | tf_op jit(solution)/shard_map/all_to_all | solution.py:54
  116.8 7.1 %all_to_all.53 = f32[2,8,16]{2,0,1:T(2,128)S(1)} all-to-all(f32[2,8,16]{2,0,1:T(2,128)S(1)} %copy.43), channel_id=1, replica_groups=mesh['gx'=4,'gy'=8] {'gy'}, dimensions={1} | all-to-all | bytes 2048 | tf_op jit(solution)/shard_map/all_to_all | solution.py:55
  123.9 4.5 %all-to-all-start = ((f32[2,128,4096]{2,0,1:T(2,128)}), f32[2,128,4096]{2,0,1:T(2,128)}, u32[]{:S(2)}, u32[]{:S(2)}) async-start(f32[2,128,4096]{2,0,1:T(2,128)} %get-tuple-element.8), calls=%async_computation | async-start | bytes 8388608 | tf_op jit(solution)/shard_map/all_to_all | solution.py:53
  128.5 49.1 %all-to-all-done = f32[2,128,4096]{2,0,1:T(2,128)} async-done(((f32[2,128,4096]{2,0,1:T(2,128)}), f32[2,128,4096]{2,0,1:T(2,128)}, u32[]{:S(2)}, u32[]{:S(2)}) %all-to-all-start) | async-done | bytes 4194336 | tf_op jit(solution)/shard_map/all_to_all | solution.py:53
  177.5 6.6 %copy.40 = f32[8,2,16,4096]{3,2,1,0:T(8,128)} copy(f32[8,2,16,4096]{3,1,2,0:T(2,128)} %bitcast.14) | data formatting | bytes 8388608 | tf_op jit(solution)/shard_map/all_to_all | solution.py:53
  184.1 0.6 copy.66
  184.7 0.6 copy.67
  (10 shorter events, 0.1 us)
Async XLA Ops:
  0.6 15.8 %copy-start = (s32[2,128]{1,0:T(2,128)S(1)}, s32[2,128]{1,0:T(2,128)}, u32[]{:S(2)}) copy-start(s32[2,128]{1,0:T(2,128)} %param.12) | copy-start | bytes 3076
  107.4 9.5 %all-to-all-start.1 = ((f32[2,8,16]{2,0,1:T(2,128)}), f32[2,8,16]{2,0,1:T(2,128)S(1)}, u32[]{:S(2)}, u32[]{:S(2)}) async-start(f32[2,8,16]{2,0,1:T(2,128)} %copy.42), calls=%async_computation.1 | async-start | bytes 16384 | tf_op jit(solution)/shard_map/all_to_all | solution.py:54
  123.9 53.7 %all-to-all-start = ((f32[2,128,4096]{2,0,1:T(2,128)}), f32[2,128,4096]{2,0,1:T(2,128)}, u32[]{:S(2)}, u32[]{:S(2)}) async-start(f32[2,128,4096]{2,0,1:T(2,128)} %get-tuple-element.8), calls=%async_computation | async-start | bytes 8388608 | tf_op jit(solution)/shard_map/all_to_all | solution.py:53
